TPU v7x, 512 devices: a whole 4x4x16 slice. The times are simulated.
512 devices in a mesh: space: 128 (over y, z, core), level: 4 (over x).
Axes of the slice: x: 4, y: 4, z: 16, core: 2. Of those that a mesh axis runs over, the one named last changes fastest.
Arguments:
- grid_latent: bfloat16 [65536, 512], P('space'), may hold values from -6 to 6
- mesh_latent: bfloat16 [4, 1024, 512], P('level', 'space'), may hold values from -6 to 6
- grid_output_cotangent: bfloat16 [65536, 512], P('space'), may hold values from -6 to 6
- w_send: bfloat16 [512, 512], replicated, may hold values from -0.25 to 0.25
- w_recv: bfloat16 [512, 512], replicated, may hold values from -0.25 to 0.25
- output_weight: bfloat16 [512, 512], replicated, may hold values from -0.25 to 0.25
- hidden_layer_bias: float32 [512], replicated, may hold values from -4 to 4
- output_norm_gain: float32 [512], replicated, may hold values from 0.1 to 1.9
- edge_sender: int32 [4, 262144], P('level', 'space'), may hold values from 0 to 23
- edge_receiver: int32 [4, 262144], P('level', 'space'), may hold values from 0 to 511
- edge_live: int32 [4, 262144], P('level', 'space'), may hold values 0 or 1
Outputs:
- d_grid: float32 [65536, 512], P(('space', 'level'))
- d_mesh: float32 [4, 1024, 512], P('level', 'space')
- d_w_send: bfloat16 [512, 512], replicated
- d_w_recv: bfloat16 [512, 512], replicated
- d_w_out: bfloat16 [512, 512], replicated
- d_bias: float32 [512], replicated
- d_gain: float32 [512], replicated
All inputs are finite; a program needn't handle non-finite values. No bound on the sum of `edge_live` on one device may be relied on, other than what follows from the above.
Results may differ from a plain program's by a relative error of at most 0.012.
Values may be sent and summed in bfloat16 or wider, within the bound.
A program may use at most 64 MiB of HBM per device.

v0:
```python
import jax
import jax.numpy as jnp
from jax import lax
from jax.sharding import PartitionSpec as P


def with_halo(cells, sides, width):
    for axis, dim in sides:
        count = lax.axis_size(axis)
        ends = count - 1
        head = lax.slice_in_dim(cells, 0, width, axis=dim)
        tail = lax.slice_in_dim(cells, cells.shape[dim] - width, cells.shape[dim], axis=dim)
        cells = jnp.concatenate(
            [
                lax.ppermute(tail, axis, [(i, (i + 1) % count) for i in range(ends)]),
                cells,
                lax.ppermute(head, axis, [((i + 1) % count, i) for i in range(ends)]),
            ],
            axis=dim,
        )
    return cells


def from_behind(block, axis, distance):
    devices = range(lax.axis_size(axis))
    route = [(i - distance, i) for i in devices if i - distance in devices]
    return lax.ppermute(block, axis, route)


def in_blocks(value, dim, peers):
    before, after = (value.shape[:dim], value.shape[dim + 1 :])
    return jnp.moveaxis(value.reshape(*before, peers, -1, *after), dim, 0)


def summed_on_arrival(value, axis, dim):
    peers = lax.axis_size(axis)
    tiles = lax.all_to_all(in_blocks(value, dim, peers), axis, 0, 0, tiled=True)
    return jnp.sum(tiles.astype(jnp.float32), axis=0)


def edge_reverse_step(
    sending_rows,
    receiver_rows,
    cotangent_lines,
    slot_active_flags,
    output_weight,
    hidden_layer_bias,
    output_norm_gain,
):
    preact = sending_rows + receiver_rows + hidden_layer_bias
    hidden = jax.nn.silu(preact).astype(jnp.bfloat16)
    outer = jnp.dot(hidden, output_weight, preferred_element_type=jnp.float32)
    center = outer - jnp.mean(outer, axis=-1, keepdims=True)
    inv_scale = lax.rsqrt(jnp.mean(center * center, axis=-1, keepdims=True) + 1e-05)
    normed = center * inv_scale
    incoming_gradient = cotangent_lines.astype(jnp.float32) * slot_active_flags[:, None].astype(
        jnp.float32
    )
    scaled = incoming_gradient * output_norm_gain
    d_outer = inv_scale * (
        scaled
        - jnp.mean(scaled, axis=-1, keepdims=True)
        - normed * jnp.mean(scaled * normed, axis=-1, keepdims=True)
    )
    d_outer_b = d_outer.astype(jnp.bfloat16)
    w_out_grad = jnp.dot(hidden.T, d_outer_b, preferred_element_type=jnp.float32)
    d_hidden = jnp.dot(d_outer_b, output_weight.T, preferred_element_type=jnp.float32)
    sigmoid = jax.nn.sigmoid(preact)
    preactivation_gradient = d_hidden * sigmoid * (1.0 + preact * (1.0 - sigmoid))
    return (
        preactivation_gradient,
        w_out_grad,
        jnp.sum(preactivation_gradient, axis=0),
        jnp.sum(incoming_gradient * normed, axis=0),
    )


def body(
    grid_latent,
    mesh_latent,
    grid_output_cotangent,
    w_send,
    w_recv,
    output_weight,
    hidden_layer_bias,
    output_norm_gain,
    edge_sender,
    edge_receiver,
    edge_live,
):
    shards = lax.axis_size("space")
    width = grid_latent.shape[1]
    grid_rows = grid_latent.shape[0]
    mesh_rows = mesh_latent.shape[1]
    slots = edge_sender.shape[1]
    sender_local = edge_sender[0]
    receiver_index = edge_receiver[0]
    band = lax.axis_index("space")
    window = sender_local // mesh_rows
    target = band + window - 1
    inside = (target >= 0) & (target < shards)
    window = jnp.where(inside, window, 1)
    table_row = window * mesh_rows + sender_local % mesh_rows
    proj_send = jnp.dot(mesh_latent[0], w_send, preferred_element_type=jnp.float32).astype(
        jnp.bfloat16
    )
    projected_receiver = jnp.dot(grid_latent, w_recv, preferred_element_type=jnp.float32)
    table = with_halo(proj_send, (("space", 0),), mesh_rows)
    sending_rows = table[table_row]
    block = 512
    blocks = slots // block

    def run_block(operands):
        rows_send, rows_recv, rows_cot, rows_live = operands
        return edge_reverse_step(
            rows_send.astype(jnp.float32),
            rows_recv,
            rows_cot,
            rows_live,
            output_weight,
            hidden_layer_bias,
            output_norm_gain,
        )

    operands = (
        sending_rows.reshape(blocks, block, width),
        projected_receiver[receiver_index].reshape(blocks, block, width),
        grid_output_cotangent[receiver_index].reshape(blocks, block, width),
        edge_live[0].reshape(blocks, block),
    )
    d_pre_blocks, wout_blocks, bias_blocks, gain_blocks = lax.map(run_block, operands)
    preactivation_gradient = d_pre_blocks.reshape(slots, width)
    output_weight_piece = jnp.sum(wout_blocks, axis=0)
    bias_piece = jnp.sum(bias_blocks, axis=0)
    gain_piece = jnp.sum(gain_blocks, axis=0)
    table_grads = jax.ops.segment_sum(preactivation_gradient, table_row, num_segments=3 * mesh_rows)
    below = table_grads[:mesh_rows]
    above = table_grads[2 * mesh_rows :]
    from_below = from_behind(above, "space", 1)
    from_above = from_behind(below, "space", -1)
    mesh_acc = table_grads[mesh_rows : 2 * mesh_rows] + from_below + from_above
    grid_local = jax.ops.segment_sum(preactivation_gradient, receiver_index, num_segments=grid_rows)
    share = grid_rows // lax.axis_size("level")
    offset = lax.axis_index("level") * share
    grid_acc = summed_on_arrival(grid_local.astype(jnp.bfloat16), "level", 0)
    grid_part = lax.dynamic_slice_in_dim(grid_latent, offset, share, 0)
    mesh_sum = mesh_acc.astype(jnp.bfloat16)
    grid_sum = grid_acc.astype(jnp.bfloat16)
    d_mesh = jnp.dot(mesh_sum, w_send.T, preferred_element_type=jnp.float32)[None]
    d_grid = jnp.dot(grid_sum, w_recv.T, preferred_element_type=jnp.float32)
    wsend_part = jnp.dot(mesh_latent[0].T, mesh_sum, preferred_element_type=jnp.float32)
    wrecv_part = jnp.dot(grid_part.T, grid_sum, preferred_element_type=jnp.float32)
    totals = lax.psum(
        (wsend_part, wrecv_part, output_weight_piece, bias_piece, gain_piece), ("space", "level")
    )
    d_w_send = totals[0].astype(jnp.bfloat16)
    d_w_recv = totals[1].astype(jnp.bfloat16)
    d_w_out = totals[2].astype(jnp.bfloat16)
    d_bias = totals[3]
    d_gain = totals[4]
    return (d_grid, d_mesh, d_w_send, d_w_recv, d_w_out, d_bias, d_gain)


def solution(mesh):
    return jax.shard_map(
        body,
        mesh=mesh,
        in_specs=(
            P("space", None),
            P("level", "space", None),
            P("space", None),
            P(),
            P(),
            P(),
            P(),
            P(),
            P("level", "space"),
            P("level", "space"),
            P("level", "space"),
        ),
        out_specs=(P(("space", "level"), None), P("level", "space", None), P(), P(), P(), P(), P()),
        check_vma=False,
    )
```

profile of v0, /device:TPU:8, one launch (start us, length us, event | category | flops | bytes accessed | tf_op | source)
XLA Modules:
  0.0 321.0 jit_solution(17864061252349421439)
XLA Ops:
  1.9 10.7 %collective-permute-start.1 = (bf16[8,512]{1,0:T(8,128)(2,1)S(1)}, bf16[8,512]{1,0:T(8,128)(2,1)S(1)}, u32[]{:S(2)}, u32[]{:S(2)}) collective-permute-start(bf16[8,512]{1,0:T(8,128)(2,1)S(1)} %convolution_convert_fusion), channel_id=1, source_target_pairs={{4,0},{8,4},{12,8},{16,12},{20,16},{24,20},{28,24},{32,28},{36,32}... | collective-permute-start | bytes 24584 | tf_op jit(solution)/shard_map/ppermute | solution.py:17
  12.7 1.9 collective-permute-start
  16.1 1.6 fusion.27
  19.7 9.2 %gather_fusion.2 = bf16[2048,512]{1,0:T(8,128)(2,1)} fusion(bf16[512,512]{1,0:T(8,128)(2,1)S(1)} %copy-done, s32[2048]{0:T(1024)S(1)} %broadcast_clamp_fusion), kind=kCustom, calls=%fused_computation.2 | custom fusion | bytes 4202496 | tf_op jit(solution)/shard_map/gather | solution.py:128
  28.9 8.9 %gather_fusion.1 = f32[2048,512]{1,0:T(8,128)} fusion(f32[512,512]{1,0:T(8,128)S(1)} %fusion.27, s32[2048]{0:T(1024)S(1)} %broadcast_clamp_fusion), kind=kCustom, calls=%fused_computation.1 | custom fusion | bytes 8396800 | tf_op jit(solution)/shard_map/gather | solution.py:127
  37.8 9.2 %gather_fusion = bf16[2048,512]{1,0:T(8,128)(2,1)} fusion(bf16[24,512]{1,0:T(8,128)(2,1)S(1)} %pad_maximum_fusion, s32[2048]{0:T(1024)S(1)} %broadcast_clamp_fusion.1), kind=kCustom, calls=%fused_computation | custom fusion | bytes 4202496 | tf_op jit(solution)/shard_map/gather | solution.py:109
  47.0 37.2 %while.16 = (s32[]{:T(128)}, f32[4,512,512]{2,1,0:T(8,128)}, f32[4,512,512]{2,1,0:T(8,128)}, f32[4,512]{1,0:T(4,128)S(1)}, f32[4,512]{1,0:T(4,128)S(1)}, /*index...) while((s32[]{:T(128)}, f32[4,512,512]{2,1,0:T(8,128)}, ...), condition=%wide.region_7.8_spmd, body=%wide.region_0.7_spmd.sunk | while | flops 816840704 | bytes 18942132 | solution.py:131
  47.0 1.7 multiply_convert_fusion.2
  51.6 1.6 fusion.63
  53.2 3.0 bitcast_dynamic-update-slice_fusion.2
  56.4 1.7 multiply_convert_fusion.2
  62.4 3.1 bitcast_dynamic-update-slice_fusion.2
  65.7 1.7 multiply_convert_fusion.2
  71.7 3.1 bitcast_dynamic-update-slice_fusion.2
  75.0 1.7 multiply_convert_fusion.2
  81.0 3.0 bitcast_dynamic-update-slice_fusion.2
  84.2 13.2 %scatter_custom_fusion.1 = f32[24,512]{1,0:T(8,128)S(1)} fusion(s32[2048]{0:T(1024)S(1)} %bitcast.107, f32[2048,512]{1,0:T(8,128)} %bitcast.109, f32[]{:T(128)} %constant.77.clone.1), kind=kCustom, calls=%fused_computation.45 | custom fusion | flops 1048576 | bytes 49664 | tf_op jit(solution)/shard_map/scatter-add | solution.py:136
  97.4 1.9 collective-permute-start.2
  99.4 5.8 %collective-permute-start.3 = (f32[8,512]{1,0:T(8,128)S(1)}, f32[8,512]{1,0:T(8,128)S(1)}, u32[]{:S(2)}, u32[]{:S(2)}) collective-permute-start(f32[8,512]{1,0:T(8,128)S(1)} %get-tuple-element.174), channel_id=1, source_target_pairs={{4,0},{8,4},{12,8},{16,12},{20,16},{24,20},{28,24},{32,28},{36,32}... | collective-permute-start | bytes 49160 | tf_op jit(solution)/shard_map/ppermute | solution.py:27
  105.2 3.8 %reduce_sum.94 = f32[512,512]{1,0:T(8,128)} reduce(f32[4,512,512]{2,1,0:T(8,128)} %get-tuple-element.73, f32[]{:T(128)} %constant.77.clone.1), dimensions={0}, to_apply=%region_13.14 | reduce | flops 786432 | bytes 5242884 | tf_op jit(solution)/shard_map/reduce_sum | solution.py:133
  109.0 13.7 %scatter_custom_fusion = f32[512,512]{1,0:T(8,128)S(1)} fusion(s32[2048]{0:T(1024)} %bitcast.108, f32[2048,512]{1,0:T(8,128)} %bitcast.110, f32[]{:T(128)} %constant.77.clone.1), kind=kCustom, calls=%fused_computation.35 | custom fusion | flops 1048576 | bytes 1049088 | tf_op jit(solution)/shard_map/scatter-add | solution.py:142
  123.6 4.3 %all-to-all-start = ((bf16[4,128,512]{2,1,0:T(8,128)(2,1)}), bf16[4,128,512]{2,1,0:T(8,128)(2,1)S(1)}, u32[]{:S(2)}, u32[]{:S(2)}) async-start(bf16[4,128,512]{2,1,0:T(8,128)(2,1)} %bitcast.17), calls=%async_computation | async-start | bytes 1048576 | tf_op jit(solution)/shard_map/all_to_all | solution.py:37
  129.1 6.8 %all-to-all-done = bf16[4,128,512]{2,1,0:T(8,128)(2,1)S(1)} async-done(((bf16[4,128,512]{2,1,0:T(8,128)(2,1)}), bf16[4,128,512]{2,1,0:T(8,128)(2,1)S(1)}, u32[]{:S(2)}, u32[]{:S(2)}) %all-to-all-start) | async-done | bytes 524320 | tf_op jit(solution)/shard_map/all_to_all | solution.py:37
  138.3 181.7 %all-reduce.2 = (bf16[512,512]{0,1:T(8,128)(2,1)S(1)}, bf16[512,512]{1,0:T(8,128)(2,1)}, bf16[512,512]{1,0:T(8,128)(2,1)}, f32[512]{0:T(512)}, f32[512]{0:T(512)}) all-reduce(f32[512,512]{0,1:T(8,128)S(1)} %convolution_bitcast_fusion.1, f32[512,512]{1,0:T(8,128)S(1)} %fusion.14, ...), channel_id=1, replica_groups=mesh['space'=128,'level'=4] {'space','level'}, use_global_device_ids=true, to_apply=%region_11.12 | all-reduce | flops 787456 | bytes 4726784 | tf_op jit(solution)/shard_map/psum | solution.py:153
  (97 shorter events, 26.6 us)
Async XLA Ops:
  0.6 19.1 %copy-start = (bf16[512,512]{1,0:T(8,128)(2,1)S(1)}, bf16[512,512]{1,0:T(8,128)(2,1)}, u32[]{:S(2)}) copy-start(bf16[512,512]{1,0:T(8,128)(2,1)} %param.15) | copy-start | bytes 1572868
  1.9 35.8 %collective-permute-start.1 = (bf16[8,512]{1,0:T(8,128)(2,1)S(1)}, bf16[8,512]{1,0:T(8,128)(2,1)S(1)}, u32[]{:S(2)}, u32[]{:S(2)}) collective-permute-start(bf16[8,512]{1,0:T(8,128)(2,1)S(1)} %convolution_convert_fusion), channel_id=1, source_target_pairs={{4,0},{8,4},{12,8},{16,12},{20,16},{24,20},{28,24},{32,28},{36,32}... | collective-permute-start | bytes 24584 | tf_op jit(solution)/shard_map/ppermute | solution.py:17
  12.7 25.1 %collective-permute-start = (bf16[8,512]{1,0:T(8,128)(2,1)S(1)}, bf16[8,512]{1,0:T(8,128)(2,1)S(1)}, u32[]{:S(2)}, u32[]{:S(2)}) collective-permute-start(bf16[8,512]{1,0:T(8,128)(2,1)S(1)} %convolution_convert_fusion), channel_id=1, source_target_pairs={{0,4},{4,8},{8,12},{12,16},{16,20},{20,24},{24,28},{28,32},{32,36}... | collective-permute-start | bytes 24584 | tf_op jit(solution)/shard_map/ppermute | solution.py:15
  37.8 9.2 %copy-start.1 = (bf16[512,512]{1,0:T(8,128)(2,1)S(1)}, bf16[512,512]{1,0:T(8,128)(2,1)}, u32[]{:S(2)}) copy-start(bf16[512,512]{1,0:T(8,128)(2,1)} %param.18) | copy-start | bytes 1572868
  37.8 9.2 %copy-start.4 = (f32[512]{0:T(512)S(1)}, f32[512]{0:T(512)}, u32[]{:S(2)}) copy-start(f32[512]{0:T(512)} %param.20) | copy-start | bytes 6148
  37.8 9.2 %copy-start.5 = (f32[512]{0:T(512)S(1)}, f32[512]{0:T(512)}, u32[]{:S(2)}) copy-start(f32[512]{0:T(512)} %param.19) | copy-start | bytes 6148
  97.4 30.4 %collective-permute-start.2 = (f32[8,512]{1,0:T(8,128)S(1)}, f32[8,512]{1,0:T(8,128)S(1)}, u32[]{:S(2)}, u32[]{:S(2)}) collective-permute-start(f32[8,512]{1,0:T(8,128)S(1)} %get-tuple-element.173), channel_id=1, source_target_pairs={{0,4},{4,8},{8,12},{12,16},{16,20},{20,24},{24,28},{28,32},{32,36}... | collective-permute-start | bytes 49160 | tf_op jit(solution)/shard_map/ppermute | solution.py:27
  99.4 28.5 %collective-permute-start.3 = (f32[8,512]{1,0:T(8,128)S(1)}, f32[8,512]{1,0:T(8,128)S(1)}, u32[]{:S(2)}, u32[]{:S(2)}) collective-permute-start(f32[8,512]{1,0:T(8,128)S(1)} %get-tuple-element.174), channel_id=1, source_target_pairs={{4,0},{8,4},{12,8},{16,12},{20,16},{24,20},{28,24},{32,28},{36,32}... | collective-permute-start | bytes 49160 | tf_op jit(solution)/shard_map/ppermute | solution.py:27
  105.2 22.7 %copy-start.6 = (bf16[1,8,512]{2,1,0:T(8,128)(2,1)S(1)}, bf16[1,8,512]{2,1,0:T(8,128)(2,1)}, u32[]{:S(2)}) copy-start(bf16[1,8,512]{2,1,0:T(8,128)(2,1)} %param.14) | copy-start | bytes 24580
  105.2 23.1 %copy-start.2 = (bf16[512,512]{1,0:T(8,128)(2,1)S(1)}, bf16[512,512]{1,0:T(8,128)(2,1)}, u32[]{:S(2)}) copy-start(bf16[512,512]{1,0:T(8,128)(2,1)} %param.16) | copy-start | bytes 1572868
  109.0 27.0 %copy-start.3 = (bf16[512,512]{1,0:T(8,128)(2,1)S(1)}, bf16[512,512]{1,0:T(8,128)(2,1)}, u32[]{:S(2)}) copy-start(bf16[512,512]{1,0:T(8,128)(2,1)} %param.17) | copy-start | bytes 1572868
  123.6 12.4 %all-to-all-start = ((bf16[4,128,512]{2,1,0:T(8,128)(2,1)}), bf16[4,128,512]{2,1,0:T(8,128)(2,1)S(1)}, u32[]{:S(2)}, u32[]{:S(2)}) async-start(bf16[4,128,512]{2,1,0:T(8,128)(2,1)} %bitcast.17), calls=%async_computation | async-start | bytes 1048576 | tf_op jit(solution)/shard_map/all_to_all | solution.py:37
where the time goes:
time: 322 us; the launch traced here: 321 us
  blocking collectives  182 us (57%)
  other arithmetic  45.8 us (14%)
  local copies, waits for them, and re-layouts  34.4 us (11%)
  matrix products  26.5 us (8%)
  starting transfers between devices  24.6 us (8%)
  waiting for transfers between devices  6.85 us (2%)
    psum x1, blocking collectives, body(): lax.psum((wsend_part, wrecv_part, output_weight_piece, bias_piece, gain_p...  182 us
    scatter-add x1, other arithmetic, body(): jax.ops.segment_sum(preactivation_gradient, receiver_index, num_segments=...  13.7 us
    scatter-add x1, other arithmetic, body(): jax.ops.segment_sum(preactivation_gradient, table_row, num_segments=3 * m...  13.2 us
    dot_general x4, matrix products, edge_reverse_step(): jnp.dot(d_outer_b, output_weight.T, preferred_element_type=jnp.float32)  12.2 us
    ppermute x1, starting transfers between devices, with_halo(): lax.ppermute(head, axis, [((i + 1) % count, i) for i in range(ends)])  10.7 us
    gather x1, local copies, waits for them, and re-layouts, body(): sending_rows = table[table_row]  9.18 us
    gather x1, local copies, waits for them, and re-layouts, body(): grid_output_cotangent[receiver_index].reshape(blocks, block, width)  9.15 us
    gather x1, local copies, waits for them, and re-layouts, body(): projected_receiver[receiver_index].reshape(blocks, block, width)  8.9 us
  transfers between devices with their start and end apart: 5, of which 1 were waited for; matrix products, arithmetic and copies ran while one was open for 13% of the time, Pallas kernels for 0%

commit v1 on v0

--- a/solution.py
+++ b/solution.py
@@ -151,7 +151,8 @@
     wsend_part = jnp.dot(mesh_latent[0].T, mesh_sum, preferred_element_type=jnp.float32)
     wrecv_part = jnp.dot(grid_part.T, grid_sum, preferred_element_type=jnp.float32)
     totals = lax.psum(
-        (wsend_part, wrecv_part, output_weight_piece, bias_piece, gain_piece), ("space", "level")
+        lax.psum((wsend_part, wrecv_part, output_weight_piece, bias_piece, gain_piece), "level"),
+        "space",
     )
     d_w_send = totals[0].astype(jnp.bfloat16)
     d_w_recv = totals[1].astype(jnp.bfloat16)

time: 322 us -> 770 us (2.39)
  the two profiles are of different devices: /device:TPU:8 before, /device:TPU:2 now
where the time goes in v1:
time: 770 us; the launch traced here: 769 us
  blocking collectives  542 us (70%)
  waiting for transfers between devices  87.2 us (11%)
  other arithmetic  45.7 us (6%)
  local copies, waits for them, and re-layouts  34.4 us (4%)
  matrix products  28.5 us (4%)
  starting transfers between devices  17 us (2%)
  between operations  14.3 us (2%)
    psum x1, blocking collectives, body(): lax.psum(lax.psum((wsend_part, wrecv_part, output_weight_piece, bias_piec...  533 us
    psum x1, waiting for transfers between devices, body(): lax.psum((wsend_part, wrecv_part, output_weight_piece, bias_piece, gain_p...  79.2 us
  transfers between devices with their start and end apart: 6, of which 2 were waited for; matrix products, arithmetic and copies ran while one was open for 6% of the time, Pallas kernels for 0%

profile of v1, /device:TPU:2, one launch (start us, length us, event | category | flops | bytes accessed | tf_op | source)
XLA Modules:
  0.0 769.2 jit_solution(7721909442522616770)
XLA Ops:
  9.8 3.0 collective-permute-start
  14.3 1.6 fusion.27
  17.9 9.2 %gather_fusion.2 = bf16[2048,512]{1,0:T(8,128)(2,1)} fusion(bf16[512,512]{1,0:T(8,128)(2,1)S(1)} %copy-done, s32[2048]{0:T(1024)S(1)} %broadcast_clamp_fusion), kind=kCustom, calls=%fused_computation.2 | custom fusion | bytes 4202496 | tf_op jit(solution)/shard_map/gather | solution.py:128
  27.1 8.9 %gather_fusion.1 = f32[2048,512]{1,0:T(8,128)} fusion(f32[512,512]{1,0:T(8,128)S(1)} %fusion.27, s32[2048]{0:T(1024)S(1)} %broadcast_clamp_fusion), kind=kCustom, calls=%fused_computation.1 | custom fusion | bytes 8396800 | tf_op jit(solution)/shard_map/gather | solution.py:127
  36.0 9.2 %gather_fusion = bf16[2048,512]{1,0:T(8,128)(2,1)} fusion(bf16[24,512]{1,0:T(8,128)(2,1)S(1)} %pad_maximum_fusion, s32[2048]{0:T(1024)S(1)} %broadcast_clamp_fusion.1), kind=kCustom, calls=%fused_computation | custom fusion | bytes 4202496 | tf_op jit(solution)/shard_map/gather | solution.py:109
  45.2 37.2 %while.16 = (s32[]{:T(128)}, f32[4,512,512]{2,1,0:T(8,128)}, f32[4,512,512]{2,1,0:T(8,128)}, f32[4,512]{1,0:T(4,128)S(1)}, f32[4,512]{1,0:T(4,128)S(1)}, /*index...) while((s32[]{:T(128)}, f32[4,512,512]{2,1,0:T(8,128)}, ...), condition=%wide.region_7.8_spmd, body=%wide.region_0.7_spmd.sunk | while | flops 816840704 | bytes 18942132 | solution.py:131
  45.2 1.7 multiply_convert_fusion.2
  51.4 3.0 bitcast_dynamic-update-slice_fusion.2
  54.6 1.7 multiply_convert_fusion.2
  60.6 3.1 bitcast_dynamic-update-slice_fusion.2
  63.9 1.7 multiply_convert_fusion.2
  69.9 3.1 bitcast_dynamic-update-slice_fusion.2
  73.2 1.7 multiply_convert_fusion.2
  79.2 3.0 bitcast_dynamic-update-slice_fusion.2
  82.4 13.2 %scatter_custom_fusion.1 = f32[24,512]{1,0:T(8,128)S(1)} fusion(s32[2048]{0:T(1024)S(1)} %bitcast.107, f32[2048,512]{1,0:T(8,128)} %bitcast.109, f32[]{:T(128)} %constant.77.clone.1), kind=kCustom, calls=%fused_computation.45 | custom fusion | flops 1048576 | bytes 49664 | tf_op jit(solution)/shard_map/scatter-add | solution.py:136
  95.6 3.4 collective-permute-start.2
  100.4 3.8 reduce_sum.94
  104.2 13.7 %scatter_custom_fusion = f32[512,512]{1,0:T(8,128)S(1)} fusion(s32[2048]{0:T(1024)} %bitcast.108, f32[2048,512]{1,0:T(8,128)} %bitcast.110, f32[]{:T(128)} %constant.77.clone.1), kind=kCustom, calls=%fused_computation.35 | custom fusion | flops 1048576 | bytes 1049088 | tf_op jit(solution)/shard_map/scatter-add | solution.py:142
  118.7 7.9 %all-to-all-start = ((bf16[4,128,512]{2,1,0:T(8,128)(2,1)}), bf16[4,128,512]{2,1,0:T(8,128)(2,1)S(1)}, u32[]{:S(2)}, u32[]{:S(2)}) async-start(bf16[4,128,512]{2,1,0:T(8,128)(2,1)} %bitcast.17), calls=%async_computation | async-start | bytes 1048576 | tf_op jit(solution)/shard_map/all_to_all | solution.py:37
  128.0 7.9 %all-to-all-done = bf16[4,128,512]{2,1,0:T(8,128)(2,1)S(1)} async-done(((bf16[4,128,512]{2,1,0:T(8,128)(2,1)}), bf16[4,128,512]{2,1,0:T(8,128)(2,1)S(1)}, u32[]{:S(2)}, u32[]{:S(2)}) %all-to-all-start) | async-done | bytes 524320 | tf_op jit(solution)/shard_map/all_to_all | solution.py:37
  136.0 2.2 fusion.14
  138.3 9.2 %all-reduce.1 = (f32[512]{0:T(512)S(1)}, f32[512]{0:T(512)S(1)}) all-reduce(f32[512]{0:T(512)S(1)} %reduce_sum.95, f32[512]{0:T(512)S(1)} %reduce_sum.96), channel_id=1, replica_groups=mesh['space'=128,'level'=4] {'level'}, use_global_device_ids=true, to_apply=%region_19.20 | all-reduce | flops 1024 | bytes 8192 | tf_op jit(solution)/shard_map/psum | solution.py:154
  149.4 79.2 %all-reduce.6.cloned.1.call-done = (f32[512,512]{0,1:T(8,128)}, f32[512,512]{1,0:T(8,128)}, f32[512,512]{1,0:T(8,128)}) async-done(((f32[512,512]{0,1:T(8,128)}, f32[512,512]{1,0:T(8,128)}, f32[512,512]{1,0:T(8,128)}), (f32[512,512]{0,1:T(8,128)}, f32[512,512]{1,0:T(8,128)}, f32[512,512]{1,0:T(8,128)})) %all-reduce.6.cloned.1.call-update) | async-done | bytes 3145744 | tf_op jit(solution)/shard_map/psum | solution.py:154
  228.6 532.7 %all-reduce.7 = (bf16[512,512]{0,1:T(8,128)(2,1)S(1)}, bf16[512,512]{1,0:T(8,128)(2,1)}, bf16[512,512]{1,0:T(8,128)(2,1)}, f32[512]{0:T(512)}, f32[512]{0:T(512)}) all-reduce(f32[512,512]{0,1:T(8,128)} %get-tuple-element.167, f32[512,512]{1,0:T(8,128)} %get-tuple-element.168, ...), channel_id=1, replica_groups=mesh['space'=128,'level'=4] {'space'}, use_global_device_ids=true, to_apply=%region_12.13 | all-reduce | flops 787456 | bytes 4726784 | tf_op jit(solution)/shard_map/psum | solution.py:153
  (101 shorter events, 30.6 us)
Async XLA Ops:
  7.2 10.7 %copy-start = (bf16[512,512]{1,0:T(8,128)(2,1)S(1)}, bf16[512,512]{1,0:T(8,128)(2,1)}, u32[]{:S(2)}) copy-start(bf16[512,512]{1,0:T(8,128)(2,1)} %param.15) | copy-start | bytes 1572868
  8.5 27.5 %collective-permute-start.1 = (bf16[8,512]{1,0:T(8,128)(2,1)S(1)}, bf16[8,512]{1,0:T(8,128)(2,1)S(1)}, u32[]{:S(2)}, u32[]{:S(2)}) collective-permute-start(bf16[8,512]{1,0:T(8,128)(2,1)S(1)} %convolution_convert_fusion), channel_id=1, source_target_pairs={{4,0},{8,4},{12,8},{16,12},{20,16},{24,20},{28,24},{32,28},{36,32}... | collective-permute-start | bytes 24584 | tf_op jit(solution)/shard_map/ppermute | solution.py:17
  9.8 26.2 %collective-permute-start = (bf16[8,512]{1,0:T(8,128)(2,1)S(1)}, bf16[8,512]{1,0:T(8,128)(2,1)S(1)}, u32[]{:S(2)}, u32[]{:S(2)}) collective-permute-start(bf16[8,512]{1,0:T(8,128)(2,1)S(1)} %convolution_convert_fusion), channel_id=1, source_target_pairs={{0,4},{4,8},{8,12},{12,16},{16,20},{20,24},{24,28},{28,32},{32,36}... | collective-permute-start | bytes 24584 | tf_op jit(solution)/shard_map/ppermute | solution.py:15
  36.0 9.2 %copy-start.1 = (bf16[512,512]{1,0:T(8,128)(2,1)S(1)}, bf16[512,512]{1,0:T(8,128)(2,1)}, u32[]{:S(2)}) copy-start(bf16[512,512]{1,0:T(8,128)(2,1)} %param.18) | copy-start | bytes 1572868
  36.0 9.2 %copy-start.4 = (f32[512]{0:T(512)S(1)}, f32[512]{0:T(512)}, u32[]{:S(2)}) copy-start(f32[512]{0:T(512)} %param.20) | copy-start | bytes 6148
  36.0 9.2 %copy-start.5 = (f32[512]{0:T(512)S(1)}, f32[512]{0:T(512)}, u32[]{:S(2)}) copy-start(f32[512]{0:T(512)} %param.19) | copy-start | bytes 6148
  95.6 31.0 %collective-permute-start.2 = (f32[8,512]{1,0:T(8,128)S(1)}, f32[8,512]{1,0:T(8,128)S(1)}, u32[]{:S(2)}, u32[]{:S(2)}) collective-permute-start(f32[8,512]{1,0:T(8,128)S(1)} %get-tuple-element.178), channel_id=1, source_target_pairs={{0,4},{4,8},{8,12},{12,16},{16,20},{20,24},{24,28},{28,32},{32,36}... | collective-permute-start | bytes 49160 | tf_op jit(solution)/shard_map/ppermute | solution.py:27
  99.1 27.6 %collective-permute-start.3 = (f32[8,512]{1,0:T(8,128)S(1)}, f32[8,512]{1,0:T(8,128)S(1)}, u32[]{:S(2)}, u32[]{:S(2)}) collective-permute-start(f32[8,512]{1,0:T(8,128)S(1)} %get-tuple-element.179), channel_id=1, source_target_pairs={{4,0},{8,4},{12,8},{16,12},{20,16},{24,20},{28,24},{32,28},{36,32}... | collective-permute-start | bytes 49160 | tf_op jit(solution)/shard_map/ppermute | solution.py:27
  100.4 26.3 %copy-start.6 = (bf16[1,8,512]{2,1,0:T(8,128)(2,1)S(1)}, bf16[1,8,512]{2,1,0:T(8,128)(2,1)}, u32[]{:S(2)}) copy-start(bf16[1,8,512]{2,1,0:T(8,128)(2,1)} %param.14) | copy-start | bytes 24580
  117.8 29.7 %copy-start.2 = (bf16[512,512]{1,0:T(8,128)(2,1)S(1)}, bf16[512,512]{1,0:T(8,128)(2,1)}, u32[]{:S(2)}) copy-start(bf16[512,512]{1,0:T(8,128)(2,1)} %param.16) | copy-start | bytes 1572868
  118.7 29.6 %copy-start.3 = (bf16[512,512]{1,0:T(8,128)(2,1)S(1)}, bf16[512,512]{1,0:T(8,128)(2,1)}, u32[]{:S(2)}) copy-start(bf16[512,512]{1,0:T(8,128)(2,1)} %param.17) | copy-start | bytes 1572868
  118.7 17.2 %all-to-all-start = ((bf16[4,128,512]{2,1,0:T(8,128)(2,1)}), bf16[4,128,512]{2,1,0:T(8,128)(2,1)S(1)}, u32[]{:S(2)}, u32[]{:S(2)}) async-start(bf16[4,128,512]{2,1,0:T(8,128)(2,1)} %bitcast.17), calls=%async_computation | async-start | bytes 1048576 | tf_op jit(solution)/shard_map/all_to_all | solution.py:37
  126.7 102.0 %all-reduce.6.cloned.1.call-start = ((), (), s32[]{:S(2)}) async-start(), calls=%async_computation.1 | async-start | bytes 6291456 | tf_op jit(solution)/shard_map/psum | solution.py:154
Sparse Core Ops, SparseCore 0:
  138.4 90.1 all-reduce.5
